TPU v7x, 32 devices: a 4x4x1 block of a 4x4x8 slice. The times are simulated.
32 devices in a mesh: dp: 1 (over z), ep: 32 (over y, x, core).
Axes of the slice: x: 4, y: 4, z: 1, core: 2. Of those that a mesh axis runs over, the one named last changes fastest.
The devices are a block of a 4x4x8 slice.
Arguments:
- x_in: bfloat16 [256, 2048], P(('dp', 'ep'))
- topk_idx: int32 [256, 8], P(('dp', 'ep'))
- topk_w: float32 [256, 8], P(('dp', 'ep'))
- w_up: bfloat16 [256, 2048, 512], P('ep')
- w_down: bfloat16 [256, 512, 2048], P('ep')
Outputs:
- output: bfloat16 [256, 2048], P(('dp', 'ep'))
All inputs are finite; a program needn't handle non-finite values.
Results may differ from a plain program's by a relative error of at most 0.00106.
Values are sent between devices in bfloat16 or wider.
A program may use at most 768 MiB of HBM per device.

v0:
```python
import jax
import jax.numpy as jnp
from jax import lax
from jax.sharding import PartitionSpec as P


def slot_layout(expert_ids, num_experts, slot_cap):
    flat_ids = expert_ids.reshape(-1)
    expert_hits = (flat_ids[:, None] == jnp.arange(num_experts, dtype=jnp.int32)[None, :]).astype(jnp.int32)
    earlier = jnp.cumsum(expert_hits, axis=0) - expert_hits
    return flat_ids * slot_cap + jnp.sum(earlier * expert_hits, axis=1)


def solution(mesh):
    group = mesh.shape['ep']
    token_spec = P(('dp', 'ep'), None)
    expert_spec = P('ep', None, None)

    def local_layer(x_loc, ids_loc, gates_loc, w_up, w_down):
        tok_n, top_n = ids_loc.shape
        model_dim = x_loc.shape[1]
        local_experts = w_up.shape[0]
        num_experts = local_experts * group
        slot_cap = tok_n // 2
        slot_ids = slot_layout(ids_loc, num_experts, slot_cap)
        slot_range = jnp.arange(num_experts * slot_cap, dtype=jnp.int32)
        placed = jnp.any(slot_ids.reshape(tok_n, top_n, 1) == slot_range, axis=1).astype(jnp.bfloat16)
        send_rows = jnp.einsum('ts,tm->sm', placed, x_loc, preferred_element_type=jnp.float32).astype(jnp.bfloat16)
        send_rows = send_rows.reshape(group, local_experts, slot_cap, model_dim)
        recv_rows = lax.all_to_all(send_rows, 'ep', 0, 2, tiled=True)
        recv_rows = recv_rows.reshape(local_experts, group * slot_cap, model_dim)
        hidden = jnp.einsum('ecm,emf->ecf', recv_rows, w_up, preferred_element_type=jnp.float32)
        hidden = jax.nn.gelu(hidden, approximate=True).astype(jnp.bfloat16)
        expert_out = jnp.einsum('ecf,efm->ecm', hidden, w_down, preferred_element_type=jnp.float32).astype(jnp.bfloat16)
        expert_out = expert_out.reshape(1, local_experts, group * slot_cap, model_dim)
        back_rows = lax.all_to_all(expert_out, 'ep', 2, 0, tiled=True)
        back_rows = back_rows.reshape(num_experts * slot_cap, model_dim)
        picked = jnp.take(back_rows, slot_ids, axis=0).reshape(tok_n, top_n, model_dim)
        mixed = jnp.sum(gates_loc[:, :, None] * picked.astype(jnp.float32), axis=1)
        return mixed.astype(jnp.bfloat16)

    return jax.shard_map(local_layer, mesh=mesh, in_specs=(token_spec, token_spec, token_spec, expert_spec, expert_spec), out_specs=token_spec, check_vma=False)
```

profile of v0, /device:TPU:103, one launch (start us, length us, event | category | flops | bytes accessed | tf_op | source)
XLA Modules:
  0.0 191.7 jit_solution(3122764493253435221)
XLA Ops:
  0.0 0.0 copy-start
  0.0 0.8 reshape.68
  0.8 0.1 fusion.14
  0.9 0.1 reduce_window_sum.11
  1.0 0.2 select_reduce_fusion
  1.1 0.1 reduce_sum.23
  1.2 0.7 compare_and_fusion
  1.9 0.2 fusion.13
  2.1 0.0 copy-done
  2.1 3.2 %convolution_convert_fusion = bf16[1024,2048]{1,0:T(8,128)(2,1)} fusion(pred[8,1024]{1,0:T(8,128)(4,1)S(1)} %fusion.13, bf16[8,2048]{1,0:T(8,128)(2,1)S(1)} %copy-done), kind=kOutput, calls=%fused_computation.3 | convolution fusion | flops 35651584 | bytes 4235264 | tf_op jit(solution)/shard_map/ts,tm->sm/dot_general | solution.py:28
  5.3 7.2 %reshape.69 = bf16[32,8,4,2048]{3,2,1,0:T(4,128)(2,1)} reshape(bf16[1024,2048]{1,0:T(8,128)(2,1)} %convolution_convert_fusion) | data formatting | bytes 8388608 | tf_op jit(solution)/shard_map/reshape | solution.py:29
  12.5 59.6 %all_to_all.30 = bf16[32,8,4,2048]{3,2,1,0:T(4,128)(2,1)S(1)} all-to-all(bf16[32,8,4,2048]{3,2,1,0:T(4,128)(2,1)} %reshape.69), channel_id=1, replica_groups=mesh['dp'=1,'ep'=32] {'ep'}, dimensions={0} | all-to-all | bytes 8388608 | tf_op jit(solution)/shard_map/all_to_all | solution.py:30
  72.1 4.0 %copy.11 = bf16[1,8,32,4,2048]{4,3,2,1,0:T(4,128)(2,1)} copy(bf16[1,8,32,4,2048]{4,3,1,2,0:T(4,128)(2,1)S(1)} %bitcast.26) | data formatting | bytes 8388608 | tf_op jit(solution)/shard_map/all_to_all | solution.py:30
  76.1 6.9 %reshape.70 = bf16[8,128,2048]{2,1,0:T(8,128)(2,1)} reshape(bf16[1,8,32,4,2048]{4,3,2,1,0:T(4,128)(2,1)} %copy.11) | data formatting | bytes 8388608 | tf_op jit(solution)/shard_map/reshape | solution.py:31
  83.0 18.8 %convert_bitcast_fusion = bf16[1,8,128,2048]{3,2,1,0:T(8,128)(2,1)} fusion(bf16[8,512,2048]{2,1,0:T(8,128)(2,1)} %param.9, bf16[8,128,2048]{2,1,0:T(8,128)(2,1)} %reshape.70, bf16[8,2048,512]{2,1,0:T(8,128)(2,1)} %param.8), kind=kOutput, calls=%fused_computation.2 | convolution fusion | flops 4301783040 | bytes 41943040 | tf_op jit(solution)/shard_map/ecf,efm->ecm/dot_general | solution.py:34
  101.8 6.5 %copy.12 = bf16[1,8,128,2048]{3,1,0,2:T(8,128)(2,1)} copy(bf16[1,8,128,2048]{3,2,1,0:T(8,128)(2,1)} %convert_bitcast_fusion) | data formatting | bytes 8388608 | tf_op jit(solution)/shard_map/reshape | solution.py:35
  108.3 6.9 %all-to-all-start.1 = ((bf16[1,8,128,2048]{3,1,0,2:T(8,128)(2,1)}), bf16[1,8,128,2048]{3,1,0,2:T(8,128)(2,1)}, u32[]{:S(2)}, u32[]{:S(2)}) async-start(bf16[1,8,128,2048]{3,1,0,2:T(8,128)(2,1)} %copy.12), calls=%async_computation.1 | async-start | bytes 8388608 | tf_op jit(solution)/shard_map/all_to_all | solution.py:36
  115.2 0.0 copy-done.2
  115.2 0.1 mul.64
  115.3 56.5 %all-to-all-done.1 = bf16[1,8,128,2048]{3,1,0,2:T(8,128)(2,1)} async-done(((bf16[1,8,128,2048]{3,1,0,2:T(8,128)(2,1)}), bf16[1,8,128,2048]{3,1,0,2:T(8,128)(2,1)}, u32[]{:S(2)}, u32[]{:S(2)}) %all-to-all-start.1) | async-done | bytes 4194336 | tf_op jit(solution)/shard_map/all_to_all | solution.py:36
  171.8 8.1 %copy.15 = bf16[1,8,32,4,2048]{4,3,1,2,0:T(4,128)(2,1)} copy(bf16[1,8,32,4,2048]{4,1,3,2,0:T(8,128)(2,1)} %bitcast.3) | data formatting | bytes 8388608 | tf_op jit(solution)/shard_map/all_to_all | solution.py:36
  180.0 6.9 %reshape.72 = bf16[1024,2048]{1,0:T(8,128)(2,1)} reshape(bf16[32,1,8,4,2048]{4,3,2,0,1:T(4,128)(2,1)} %bitcast.27) | data formatting | bytes 8388608 | tf_op jit(solution)/shard_map/reshape | solution.py:37
  186.9 3.7 %gather_fusion = bf16[64,2048]{1,0:T(8,128)(2,1)S(1)} fusion(bf16[1024,2048]{1,0:T(8,128)(2,1)} %reshape.72, s32[1024]{0:T(1024)S(1)} %pad_clamp_fusion), kind=kCustom, calls=%fused_computation | custom fusion | bytes 524544 | tf_op jit(solution)/shard_map/jit(_take)/gather | solution.py:38
  190.6 1.0 multiply_reduce_fusion
  (8 shorter events, 0.0 us)
Async XLA Ops:
  0.0 2.1 %copy-start = (bf16[8,2048]{1,0:T(8,128)(2,1)S(1)}, bf16[8,2048]{1,0:T(8,128)(2,1)}, u32[]{:S(2)}) copy-start(bf16[8,2048]{1,0:T(8,128)(2,1)} %param.5) | copy-start | bytes 98308
  108.3 6.9 %copy-start.2 = (s32[8,8]{1,0:T(8,128)S(1)}, s32[8,8]{1,0:T(8,128)}, u32[]{:S(2)}) copy-start(s32[8,8]{1,0:T(8,128)} %param.6) | copy-start | bytes 772
  108.3 63.5 %all-to-all-start.1 = ((bf16[1,8,128,2048]{3,1,0,2:T(8,128)(2,1)}), bf16[1,8,128,2048]{3,1,0,2:T(8,128)(2,1)}, u32[]{:S(2)}, u32[]{:S(2)}) async-start(bf16[1,8,128,2048]{3,1,0,2:T(8,128)(2,1)} %copy.12), calls=%async_computation.1 | async-start | bytes 8388608 | tf_op jit(solution)/shard_map/all_to_all | solution.py:36
  180.0 11.7 %copy-start.1 = (bf16[8,2048]{1,0:T(8,128)(2,1)S(1)}, bf16[8,2048]{1,0:T(8,128)(2,1)}, u32[]{:S(2)}) copy-start(bf16[8,2048]{1,0:T(8,128)(2,1)} %param.5) | copy-start | bytes 98308
  180.0 10.6 %copy-start.3 = (f32[8,8]{1,0:T(8,128)S(1)}, f32[8,8]{1,0:T(8,128)}, u32[]{:S(2)}) copy-start(f32[8,8]{1,0:T(8,128)} %param.7) | copy-start | bytes 772
where the time goes:
time: 192 us
  blocking collectives  59.6 us (31%)
  waiting for transfers between devices  56.5 us (29%)
  local copies, waits for them, and re-layouts  44.3 us (23%)
  matrix products  22 us (11%)
  starting transfers between devices  6.94 us (4%)
  other arithmetic  2.29 us (1%)
    all_to_all x1, blocking collectives, local_layer(): recv_rows = lax.all_to_all(send_rows, 'ep', 0, 2, tiled=True)  59.6 us
    all_to_all x1, waiting for transfers between devices, local_layer(): back_rows = lax.all_to_all(expert_out, 'ep', 2, 0, tiled=True)  56.5 us
    dot_general x1, matrix products, local_layer(): jnp.einsum('ecf,efm->ecm', hidden, w_down, preferred_element_type=jnp.flo...  18.8 us
    all_to_all x1, local copies, waits for them, and re-layouts, local_layer(): back_rows = lax.all_to_all(expert_out, 'ep', 2, 0, tiled=True)  8.14 us
    reshape x1, local copies, waits for them, and re-layouts, local_layer(): send_rows = send_rows.reshape(group, local_experts, slot_cap, model_dim)  7.19 us
    all_to_all x1, starting transfers between devices, local_layer(): back_rows = lax.all_to_all(expert_out, 'ep', 2, 0, tiled=True)  6.94 us
    reshape x1, local copies, waits for them, and re-layouts, local_layer(): back_rows = back_rows.reshape(num_experts * slot_cap, model_dim)  6.92 us
    reshape x1, local copies, waits for them, and re-layouts, local_layer(): recv_rows = recv_rows.reshape(local_experts, group * slot_cap, model_dim)  6.91 us
  transfers between devices with their start and end apart: 1, of which 1 were waited for; matrix products, arithmetic and copies ran while one was open for 0% of the time, Pallas kernels for 0%

commit v1 on v0

v1 whole, which is shorter than its diff:
```python
import functools
import math

import jax
import jax.numpy as jnp
from jax import lax
from jax.experimental import pallas as pl
from jax.experimental.pallas import tpu as pltpu
from jax.sharding import PartitionSpec as P

MESH = pl.DeviceIdType.MESH
LANES = 128
KC = 4
QC = 4


def moe_kernel(side, x_hbm, ids_hbm, gates_hbm, up_hbm, down_hbm, y_ref,
               up, down, gath, meta, ids_v, gates_v, rows, z, h, gate, part, pair, ring, line, cross,
               in_sem, up_sem, down_sem,
               g1_s, g1_r, g2_s, g2_r, g3_s, g3_r,
               r0_s, r0_r, r1_s, r1_r, r2_s, r2_r):
    n_exp, dim, ff = up.shape
    tok = x_hbm.shape[0]
    total = 2 * side * side * tok
    kw = dim // KC
    qw = dim // QC
    me = lax.axis_index('ep')
    core = lax.rem(me, 2)
    col = lax.rem(me // 2, side)
    row = me // (2 * side)

    def at(dy, dx, dc=0):
        return {'ep': (lax.rem(row + dy, side) * side + lax.rem(col + dx, side)) * 2 + lax.rem(core + dc, 2)}

    def neg(d):
        return (side - d) % side

    def rcopy(src, dst, ss, rs, dev):
        return pltpu.make_async_remote_copy(src_ref=src, dst_ref=dst, send_sem=ss, recv_sem=rs, device_id=dev, device_id_type=MESH)

    loads = [pltpu.make_async_copy(x_hbm.at[:, pl.ds(k * kw, kw)], gath.at[k, 0, 0, 0], in_sem.at[k]) for k in range(KC)]
    loads.append(pltpu.make_async_copy(ids_hbm, ids_v, in_sem.at[KC]))
    loads.append(pltpu.make_async_copy(gates_hbm, gates_v, in_sem.at[KC + 1]))
    for c in loads:
        c.start()

    def up_copy(k, e):
        return pltpu.make_async_copy(up_hbm.at[e, pl.ds(k * kw, kw), :], up.at[e, pl.ds(k * kw, kw), :], up_sem.at[k, e])

    def down_copy(q, e):
        return pltpu.make_async_copy(down_hbm.at[e, :, pl.ds(q * qw, qw)], down.at[e, :, pl.ds(q * qw, qw)], down_sem.at[q, e])

    for k in range(KC):
        for e in range(n_exp):
            up_copy(k, e).start()
    for q in range(QC):
        for e in range(n_exp):
            down_copy(q, e).start()

    peers = [at(0, d) for d in range(1, side)] + [at(d, 0) for d in range(1, side)] + [at(0, 0, 1)]
    barrier = pltpu.get_barrier_semaphore()
    for dev in peers:
        pl.semaphore_signal(barrier, inc=1, device_id=dev, device_id_type=MESH)

    for c in loads[KC:]:
        c.wait()
    top = ids_v.shape[1]
    meta[0, 0, 0, 0] = jnp.full((tok, LANES), -1.0, jnp.float32)
    meta[0, 0, 0, 1] = jnp.zeros((tok, LANES), jnp.float32)
    meta[0, 0, 0, 0, :, 0:top] = ids_v[...].astype(jnp.float32)
    meta[0, 0, 0, 1, :, 0:top] = gates_v[...]
    for c in loads[:KC]:
        c.wait()
    pl.semaphore_wait(barrier, len(peers))

    def block(k):
        return meta if k == KC else gath.at[k]

    def first(k, d):
        b, lane = block(k), k % 2 == 0
        dst = b.at[0, 0, neg(d)] if lane else b.at[0, neg(d), 0]
        return rcopy(b.at[0, 0, 0], dst, g1_s.at[k, d], g1_r.at[k, neg(d)], at(0, d) if lane else at(d, 0))

    def first_in(k, d):
        b, lane = block(k), k % 2 == 0
        dst = b.at[0, 0, d] if lane else b.at[0, d, 0]
        return rcopy(b.at[0, 0, 0], dst, g1_s.at[k, d], g1_r.at[k, d], at(0, d) if lane else at(d, 0))

    def second(k, d):
        b, lane = block(k), k % 2 == 0
        src = b.at[0, 0] if lane else b.at[0, :, 0]
        dst = b.at[0, neg(d)] if lane else b.at[0, :, neg(d)]
        return rcopy(src, dst, g2_s.at[k, d], g2_r.at[k, neg(d)], at(d, 0) if lane else at(0, d))

    def second_in(k, d):
        b, lane = block(k), k % 2 == 0
        src = b.at[0, 0] if lane else b.at[0, :, 0]
        dst = b.at[0, d] if lane else b.at[0, :, d]
        return rcopy(src, dst, g2_s.at[k, d], g2_r.at[k, d], at(d, 0) if lane else at(0, d))

    def third(k):
        b = block(k)
        return rcopy(b.at[0], b.at[1], g3_s.at[k], g3_r.at[k], at(0, 0, 1))

    offs = [2, 1, 3] if side == 4 else list(range(1, side))
    streams = list(range(KC + 1))
    for k in streams:
        for d in offs:
            first(k, d).start()
    for k in streams:
        for d in offs:
            first_in(k, d).wait_recv()
        for d in offs:
            second(k, d).start()
    for k in streams:
        for d in offs:
            second_in(k, d).wait_recv()
        third(k).start()

    def wide(g, n):
        return jnp.concatenate([g] * (n // LANES), axis=1)

    for k in range(KC):
        third(k).wait_recv()
        rows[k] = gath[k].astype(jnp.float32).reshape(total, kw).astype(jnp.bfloat16)
        for e in range(n_exp):
            up_copy(k, e).wait()
        if k == KC - 1:
            third(KC).wait_recv()
            ids_all = meta[:, :, :, 0].reshape(total, LANES)
            gates_all = meta[:, :, :, 1].reshape(total, LANES)
            for e in range(n_exp):
                eid = (me * n_exp + e).astype(jnp.float32)
                g = jnp.sum(jnp.where(ids_all == eid, gates_all, 0.0), axis=1, keepdims=True)
                gate[e] = jnp.broadcast_to(g, (total, LANES))
        for e in range(n_exp):
            acc = jnp.dot(rows[k], up[e, pl.ds(k * kw, kw), :], preferred_element_type=jnp.float32)
            if k > 0:
                acc = z[e] + acc
            if k < KC - 1:
                z[e] = acc
            else:
                act = jax.nn.gelu(acc, approximate=True)
                h[e] = jnp.where(wide(gate[e], ff) > 0.0, act, 0.0).astype(jnp.bfloat16)

    def pair_out(q):
        return rcopy(part.at[q, 1], pair.at[q], r0_s.at[q], r0_r.at[q], at(0, 0, 1))

    def ring_out(q, d):
        lane = q % 2 == 0
        src = part.at[q, 0, :, d] if lane else part.at[q, 0, d]
        return rcopy(src, ring.at[q, neg(d)], r1_s.at[q, d], r1_r.at[q, neg(d)], at(0, d) if lane else at(d, 0))

    def ring_in(q, d):
        lane = q % 2 == 0
        src = part.at[q, 0, :, d] if lane else part.at[q, 0, d]
        return rcopy(src, ring.at[q, d], r1_s.at[q, d], r1_r.at[q, d], at(0, d) if lane else at(d, 0))

    def cross_out(q, d):
        lane = q % 2 == 0
        return rcopy(line.at[q, d], cross.at[q, neg(d)], r2_s.at[q, d], r2_r.at[q, neg(d)], at(d, 0) if lane else at(0, d))

    def cross_in(q, d):
        lane = q % 2 == 0
        return rcopy(line.at[q, d], cross.at[q, d], r2_s.at[q, d], r2_r.at[q, d], at(d, 0) if lane else at(0, d))

    def stage1(q):
        pair_out(q).wait_recv()
        part[q, 0] = part[q, 0] + pair[q]
        for d in offs:
            ring_out(q, d).start()

    def stage2(q):
        for d in offs:
            ring_in(q, d).wait_recv()
        own = part[q, 0, :, 0] if q % 2 == 0 else part[q, 0, 0]
        for d in range(1, side):
            own = own + ring[q, d]
        line[q] = own
        for d in offs:
            cross_out(q, d).start()

    def stage3(q):
        for d in offs:
            cross_in(q, d).wait_recv()
        s = line[q, 0]
        for d in range(1, side):
            s = s + cross[q, d]
        y_ref[:, q * qw:(q + 1) * qw] = s.astype(y_ref.dtype)

    for q in range(QC):
        for e in range(n_exp):
            down_copy(q, e).wait()
        for e in range(n_exp):
            o = jnp.dot(h[e], down[e, :, pl.ds(q * qw, qw)], preferred_element_type=jnp.float32)
            o = o.astype(jnp.bfloat16).astype(jnp.float32) * wide(gate[e], qw)
            o = o.reshape(2, side, side, tok, qw)
            part[q] = o if e == 0 else part[q] + o
        pair_out(q).start()
        if q >= 1:
            stage1(q - 1)
        if q >= 3:
            stage2(q - 3)
    stage1(QC - 1)
    for q in range(QC):
        if q >= QC - 3:
            stage2(q)
    for q in range(QC):
        stage3(q)

    for k in streams:
        for d in offs:
            first(k, d).wait_send()
            second(k, d).wait_send()
        third(k).wait_send()
    for q in range(QC):
        pair_out(q).wait_send()
        for d in offs:
            ring_out(q, d).wait_send()
            cross_out(q, d).wait_send()


def solution(mesh):
    group = mesh.shape['ep']
    side = math.isqrt(group // 2)
    token_spec = P(('dp', 'ep'), None)
    expert_spec = P('ep', None, None)

    def local_layer(x_loc, ids_loc, gates_loc, w_up, w_down):
        tok, dim = x_loc.shape
        n_exp, _, ff = w_up.shape
        total = tok * group
        kw, qw = dim // KC, dim // QC
        f32, bf16 = jnp.float32, jnp.bfloat16
        dma = pltpu.SemaphoreType.DMA
        scratch = [
            pltpu.VMEM(w_up.shape, bf16),
            pltpu.VMEM(w_down.shape, bf16),
            pltpu.VMEM((KC, 2, side, side, tok, kw), bf16),
            pltpu.VMEM((2, side, side, 2, tok, LANES), f32),
            pltpu.VMEM(ids_loc.shape, jnp.int32),
            pltpu.VMEM(gates_loc.shape, f32),
            pltpu.VMEM((KC, total, kw), bf16),
            pltpu.VMEM((n_exp, total, ff), f32),
            pltpu.VMEM((n_exp, total, ff), bf16),
            pltpu.VMEM((n_exp, total, LANES), f32),
            pltpu.VMEM((QC, 2, side, side, tok, qw), f32),
            pltpu.VMEM((QC, side, side, tok, qw), f32),
            pltpu.VMEM((QC, side, side, tok, qw), f32),
            pltpu.VMEM((QC, side, tok, qw), f32),
            pltpu.VMEM((QC, side, tok, qw), f32),
            dma((KC + 2,)), dma((KC, n_exp)), dma((QC, n_exp)),
            dma((KC + 1, side)), dma((KC + 1, side)), dma((KC + 1, side)), dma((KC + 1, side)), dma((KC + 1,)), dma((KC + 1,)),
            dma((QC,)), dma((QC,)), dma((QC, side)), dma((QC, side)), dma((QC, side)), dma((QC, side)),
        ]
        return pl.pallas_call(
            functools.partial(moe_kernel, side),
            out_shape=jax.ShapeDtypeStruct((tok, dim), bf16),
            in_specs=[pl.BlockSpec(memory_space=pl.ANY)] * 5,
            out_specs=pl.BlockSpec(memory_space=pltpu.VMEM),
            scratch_shapes=scratch,
            compiler_params=pltpu.CompilerParams(collective_id=0, has_side_effects=True, vmem_limit_bytes=60 * 1024 * 1024),
        )(x_loc, ids_loc, gates_loc, w_up, w_down)

    return jax.shard_map(local_layer, mesh=mesh, in_specs=(token_spec, token_spec, token_spec, expert_spec, expert_spec), out_specs=token_spec, check_vma=False)
```

time: 192 us -> 50.1 us (0.26)
  the two profiles are of different devices: /device:TPU:103 before, /device:TPU:97 now
where the time goes in v1:
time: 50.1 us; the launch traced here: 49.5 us
  Pallas kernels  48.1 us (96%)
  local copies, waits for them, and re-layouts  1.38 us (3%)
    pallas_call x1, Pallas kernels, local_layer(): pl.pallas_call(functools.partial(moe_kernel, side), out_shape=jax.ShapeDt...  48.1 us
    unnamed x1, local copies, waits for them, and re-layouts  1.38 us

profile of v1, /device:TPU:97, one launch (start us, length us, event | category | flops | bytes accessed | tf_op | source)
XLA Modules:
  0.0 49.5 jit_solution(9726388959501061932)
XLA Ops:
  0.0 48.1 %shard_map.55 = bf16[8,2048]{1,0:T(8,128)(2,1)} custom-call(bf16[8,2048]{1,0:T(8,128)(2,1)} %x_hbm.1, s32[8,8]{1,0:T(8,128)} %ids_hbm.1, f32[8,8]{1,0:T(8,128)} %gates_hbm.1, bf16[8,2048,512]{2,1,0:T(8,128)(2,1)} %up_hbm.1, bf16[8,512,2048]{2,1,0:T(8,128)(2,1)} %down_hbm.1), custom_call_target="tpu_custom_call" | custom-call | tf_op jit(solution)/shard_map/pallas_call | solution.py:256
  48.1 1.4 %copy.7 = bf16[8,2048]{1,0:T(8,128)(2,1)} copy(bf16[8,2048]{1,0:T(8,128)(2,1)} %shard_map.55) | data formatting | bytes 65536

commit v2 on v0

v2 whole, which is shorter than its diff:
```python
import functools
import math

import jax
import jax.numpy as jnp
from jax import lax
from jax.experimental import pallas as pl
from jax.experimental.pallas import tpu as pltpu
from jax.sharding import PartitionSpec as P

MESH = pl.DeviceIdType.MESH
LANES = 128
KC = 4
QC = 4
LAG = 2


def wide(g, n):
    return jnp.concatenate([g] * (n // LANES), axis=1)


def moe_kernel(side, x_hbm, ids_hbm, gates_hbm, up_hbm, down_hbm, y_ref,
               up, down, gath, meta, ids_v, gates_v, rows, z, h, gate, part, pair, ring, line, cross,
               in_sem, up_sem, down_sem, go, ag_s, ag_r, fw_s, fw_r, pair_s, pair_r, ring_s, ring_r, cross_s, cross_r):
    n_exp, dim, ff = up.shape
    tok = x_hbm.shape[0]
    chips = side * side
    half = chips * tok
    kw = dim // KC
    qw = dim // QC
    me = lax.axis_index('ep')
    core = lax.rem(me, 2)
    col = lax.rem(me // 2, side)
    row = me // (2 * side)

    def at(dy, dx, dc=0):
        return {'ep': (lax.rem(row + dy, side) * side + lax.rem(col + dx, side)) * 2 + lax.rem(core + dc, 2)}

    def neg(d):
        return (side - d) % side

    def rcopy(src, dst, ss, rs, dev):
        return pltpu.make_async_remote_copy(src_ref=src, dst_ref=dst, send_sem=ss, recv_sem=rs, device_id=dev, device_id_type=MESH)

    partner = at(0, 0, 1)
    offs = [(dy, dx) for dy in range(side) for dx in range(side) if dy or dx]
    offs.sort(key=lambda o: -(min(o[0], side - o[0]) + min(o[1], side - o[1])))
    line_offs = sorted(range(1, side), key=lambda d: -min(d, side - d))

    x_loads = [pltpu.make_async_copy(x_hbm.at[:, pl.ds(k * kw, kw)], gath.at[k, core, 0], in_sem.at[0]) for k in range(KC)]
    loads = [pltpu.make_async_copy(ids_hbm, ids_v, in_sem.at[1]), pltpu.make_async_copy(gates_hbm, gates_v, in_sem.at[2])]
    for c in loads + x_loads:
        c.start()
    barrier = pltpu.get_barrier_semaphore()
    for dy, dx in offs:
        pl.semaphore_signal(barrier, inc=1, device_id=at(dy, dx), device_id_type=MESH)
    pl.semaphore_signal(barrier, inc=1, device_id=partner, device_id_type=MESH)
    for c in loads:
        c.wait()
    top = ids_v.shape[1]
    meta[core, 0] = jnp.full((tok, LANES), -1.0, jnp.float32)
    meta[core, 0, :, 0:top] = ids_v[...].astype(jnp.float32)
    meta[core, 0, :, LANES // 2:LANES // 2 + top] = gates_v[...]
    pltpu.make_async_copy(gath.at[:, core, 0], gath.at[:, core, 0], in_sem.at[0]).wait()

    def up_copy(k):
        return pltpu.make_async_copy(up_hbm.at[:, pl.ds(k * kw, kw), :], up.at[:, pl.ds(k * kw, kw), :], up_sem.at[k])

    def down_copy(q):
        return pltpu.make_async_copy(down_hbm.at[:, :, pl.ds(q * qw, qw)], down.at[:, :, pl.ds(q * qw, qw)], down_sem.at[q])

    for k in range(KC):
        up_copy(k).start()
    for q in range(QC):
        down_copy(q).start()
    pl.semaphore_wait(barrier, len(offs) + 1)

    def block(k):
        return meta if k == KC else gath.at[k]

    def send(k, o):
        b = block(k)
        return rcopy(b.at[core, 0], b.at[core, neg(o[0]) * side + neg(o[1])], ag_s.at[k], ag_r.at[k], at(*o))

    def gathered(k):
        b = block(k).at[core, pl.ds(1, chips - 1)]
        return rcopy(b, b, ag_s.at[k], ag_r.at[k], partner)

    def forward(k):
        b = block(k).at[core]
        return rcopy(b, b, fw_s.at[k], fw_r.at[k], partner)

    def forwarded(k):
        b = block(k).at[1 - core]
        return rcopy(b, b, fw_s.at[k], fw_r.at[k], partner)

    streams = [KC] + list(range(KC))

    @pl.when(core == 1)
    def _():
        pl.semaphore_wait(go, 1)

    for k in streams:
        for o in offs:
            send(k, o).start()

    @pl.when(core == 0)
    def _():
        for k in streams[:-1]:
            gathered(k).wait_send()
        pl.semaphore_signal(go, inc=1, device_id=partner, device_id_type=MESH)
        gathered(streams[-1]).wait_send()

    def pass_on(k):
        gathered(k).wait_recv()
        forward(k).start()

    def arrive(c, k):
        if c == 0:
            @pl.when(core == 0)
            def _():
                pass_on(k)

        @pl.when(core != c)
        def _():
            forwarded(k).wait_recv()

    def find_gates(c):
        ids_all = meta[c].reshape(half, LANES)
        gates_all = pltpu.roll(ids_all, LANES // 2, axis=1)
        lane = lax.broadcasted_iota(jnp.int32, (half, LANES), 1)
        for e in range(n_exp):
            eid = (me * n_exp + e).astype(jnp.float32)
            g = jnp.sum(jnp.where((ids_all == eid) & (lane < top), gates_all, 0.0), axis=1, keepdims=True)
            gate[c, e] = jnp.broadcast_to(g, (half, LANES))

    def up_chunk(c, k):
        rows[k] = gath[k, c].astype(jnp.float32).reshape(half, kw).astype(jnp.bfloat16)
        for e in range(n_exp):
            acc = jnp.dot(rows[k], up[e, pl.ds(k * kw, kw), :], preferred_element_type=jnp.float32)
            if k > 0:
                acc = z[e] + acc
            if k < KC - 1:
                z[e] = acc
            else:
                act = jax.nn.gelu(acc, approximate=True)
                h[e] = jnp.where(wide(gate[c, e], ff) > 0.0, act, 0.0).astype(jnp.bfloat16)

    def down_chunk(c, q):
        for e in range(n_exp):
            o = jnp.dot(h[e], down[e, :, pl.ds(q * qw, qw)], preferred_element_type=jnp.float32)
            o = o.astype(jnp.bfloat16).astype(jnp.float32) * wide(gate[c, e], qw)
            o = o.reshape(side, side, tok, qw)
            part[c, q] = o if e == 0 else part[c, q] + o

    def pair_out(c, q):
        return rcopy(part.at[c, q], pair.at[q], pair_s, pair_r.at[q], partner)

    def ring_out(c, q, d):
        lane = q % 2 == 0
        src = part.at[c, q, :, d] if lane else part.at[c, q, d]
        return rcopy(src, ring.at[q, neg(d)], ring_s, ring_r.at[q], at(0, d) if lane else at(d, 0))

    def cross_out(q, d):
        lane = q % 2 == 0
        return rcopy(line.at[q, d], cross.at[q, neg(d)], cross_s, cross_r.at[q], at(d, 0) if lane else at(0, d))

    def came(ref, ss, rs):
        return rcopy(ref, ref, ss, rs, partner)

    def stage1(c, q):
        came(pair.at[q], pair_s, pair_r.at[q]).wait_recv()
        part[c, q] = part[c, q] + pair[q]
        for d in line_offs:
            ring_out(c, q, d).start()

    def stage2(c, q):
        came(ring.at[q, pl.ds(1, side - 1)], ring_s, ring_r.at[q]).wait_recv()
        own = part[c, q, :, 0] if q % 2 == 0 else part[c, q, 0]
        for d in range(1, side):
            own = own + ring[q, d]
        line[q] = own
        for d in line_offs:
            cross_out(q, d).start()

    def stage3(q):
        came(cross.at[q, pl.ds(1, side - 1)], cross_s, cross_r.at[q]).wait_recv()
        s = line[q, 0]
        for d in range(1, side):
            s = s + cross[q, d]
        y_ref[:, q * qw:(q + 1) * qw] = s.astype(y_ref.dtype)

    arrive(0, KC)
    find_gates(0)
    for k in range(KC):
        arrive(0, k)
        up_copy(k).wait()
        up_chunk(0, k)
    pending = list(streams)

    def next_pass(n):
        ks, pending[:] = pending[:n], pending[n:]
        for k in ks:
            pass_on(k)

    @pl.when(core == 1)
    def _():
        next_pass(2)
    for q in range(QC):
        down_copy(q).wait()
        down_chunk(0, q)

        @pl.when(core == 1)
        def _():
            pair_out(0, q).start()
            next_pass(1 if q < QC - 1 else len(pending))

    arrive(1, KC)
    find_gates(1)
    for k in range(KC):
        arrive(1, k)
        up_chunk(1, k)
        if k < QC:
            @pl.when(core == 0)
            def _():
                stage1(0, k)
    for q in range(QC):
        down_chunk(1, q)

        @pl.when(core == 0)
        def _():
            pair_out(1, q).start()
            if q >= 1:
                stage2(0, q - 1)

        @pl.when(core == 1)
        def _():
            if q >= LAG:
                stage1(1, q - LAG)

    @pl.when(core == 0)
    def _():
        stage2(0, QC - 1)

    @pl.when(core == 1)
    def _():
        for q in range(QC - LAG, QC):
            stage1(1, q)
        for q in range(QC):
            stage2(1, q)
    for q in range(QC):
        stage3(q)

    @pl.when(core == 1)
    def _():
        for k in streams:
            gathered(k).wait_send()
    for k in streams:
        forward(k).wait_send()
    came(pair, pair_s, pair_r.at[0]).wait_send()
    came(ring.at[:, pl.ds(1, side - 1)], ring_s, ring_r.at[0]).wait_send()
    came(cross.at[:, pl.ds(1, side - 1)], cross_s, cross_r.at[0]).wait_send()


def solution(mesh):
    group = mesh.shape['ep']
    side = math.isqrt(group // 2)
    token_spec = P(('dp', 'ep'), None)
    expert_spec = P('ep', None, None)

    def local_layer(x_loc, ids_loc, gates_loc, w_up, w_down):
        tok, dim = x_loc.shape
        n_exp, _, ff = w_up.shape
        half = tok * group // 2
        kw, qw = dim // KC, dim // QC
        f32, bf16 = jnp.float32, jnp.bfloat16
        dma = pltpu.SemaphoreType.DMA
        scratch = [
            pltpu.VMEM(w_up.shape, bf16),
            pltpu.VMEM(w_down.shape, bf16),
            pltpu.VMEM((KC, 2, side * side, tok, kw), bf16),
            pltpu.VMEM((2, side * side, tok, LANES), f32),
            pltpu.VMEM(ids_loc.shape, jnp.int32),
            pltpu.VMEM(gates_loc.shape, f32),
            pltpu.VMEM((KC, half, kw), bf16),
            pltpu.VMEM((n_exp, half, ff), f32),
            pltpu.VMEM((n_exp, half, ff), bf16),
            pltpu.VMEM((2, n_exp, half, LANES), f32),
            pltpu.VMEM((2, QC, side, side, tok, qw), f32),
            pltpu.VMEM((QC, side, side, tok, qw), f32),
            pltpu.VMEM((QC, side, side, tok, qw), f32),
            pltpu.VMEM((QC, side, tok, qw), f32),
            pltpu.VMEM((QC, side, tok, qw), f32),
            dma((3,)), dma((KC,)), dma((QC,)), pltpu.SemaphoreType.REGULAR,
            dma((KC + 1,)), dma((KC + 1,)), dma((KC + 1,)), dma((KC + 1,)),
            dma, dma((QC,)), dma, dma((QC,)), dma, dma((QC,)),
        ]
        return pl.pallas_call(
            functools.partial(moe_kernel, side),
            out_shape=jax.ShapeDtypeStruct((tok, dim), bf16),
            in_specs=[pl.BlockSpec(memory_space=pl.ANY)] * 5,
            out_specs=pl.BlockSpec(memory_space=pltpu.VMEM),
            scratch_shapes=scratch,
            compiler_params=pltpu.CompilerParams(collective_id=0, has_side_effects=True, vmem_limit_bytes=60 * 1024 * 1024),
        )(x_loc, ids_loc, gates_loc, w_up, w_down)

    return jax.shard_map(local_layer, mesh=mesh, in_specs=(token_spec, token_spec, token_spec, expert_spec, expert_spec), out_specs=token_spec, check_vma=False)
```

time: 192 us -> 37.8 us (0.20)
  the two profiles are of different devices: /device:TPU:103 before, /device:TPU:97 now
where the time goes in v2:
time: 37.8 us; the launch traced here: 37.6 us
  Pallas kernels  36.2 us (96%)
  local copies, waits for them, and re-layouts  1.38 us (4%)
    pallas_call x1, Pallas kernels, local_layer(): pl.pallas_call(functools.partial(moe_kernel, side), out_shape=jax.ShapeDt...  36.2 us
    unnamed x1, local copies, waits for them, and re-layouts  1.38 us

profile of v2, /device:TPU:97, one launch (start us, length us, event | category | flops | bytes accessed | tf_op | source)
XLA Modules:
  0.0 37.6 jit_solution(8624807983971453166)
XLA Ops:
  0.0 36.2 %shard_map.55 = bf16[8,2048]{1,0:T(8,128)(2,1)} custom-call(bf16[8,2048]{1,0:T(8,128)(2,1)} %x_hbm.1, s32[8,8]{1,0:T(8,128)} %ids_hbm.1, f32[8,8]{1,0:T(8,128)} %gates_hbm.1, bf16[8,2048,512]{2,1,0:T(8,128)(2,1)} %up_hbm.1, bf16[8,512,2048]{2,1,0:T(8,128)(2,1)} %down_hbm.1), custom_call_target="tpu_custom_call" | custom-call | tf_op jit(solution)/shard_map/pallas_call | solution.py:298
  36.3 1.4 %copy.7 = bf16[8,2048]{1,0:T(8,128)(2,1)} copy(bf16[8,2048]{1,0:T(8,128)(2,1)} %shard_map.55) | data formatting | bytes 65536

commit v3 on v2

--- a/solution.py
+++ b/solution.py
@@ -11,17 +11,26 @@
 MESH = pl.DeviceIdType.MESH
 LANES = 128
 KC = 4
+GO = 4
 QC = 4
-LAG = 2
+PASS = ((0, 1), (2,), (3,), (4,))
+BLOCKS = (((0,), (1,), (2,), (3,)), ((0,), (1,), (2,), (3,)))
+FLAT = True
 
 
 def wide(g, n):
     return jnp.concatenate([g] * (n // LANES), axis=1)
 
 
+def gelu(v):
+    a = math.sqrt(2 / math.pi)
+    half_v = 0.5 * v
+    return half_v + half_v * jnp.tanh(v * (a + (a * 0.044715) * (v * v)))
+
+
 def moe_kernel(side, x_hbm, ids_hbm, gates_hbm, up_hbm, down_hbm, y_ref,
-               up, down, gath, meta, ids_v, gates_v, rows, z, h, gate, part, pair, ring, line, cross,
-               in_sem, up_sem, down_sem, go, ag_s, ag_r, fw_s, fw_r, pair_s, pair_r, ring_s, ring_r, cross_s, cross_r):
+               up, down, gath, meta, ids_v, gates_v, rows, z, h, gate, part, pair, ring, line, cross, flat,
+               in_sem, up_sem, down_sem, go, ag_s, ag_r, fw_s, fw_r, pair_s, pair_r, ring_s, ring_r, cross_s, cross_r, flat_s, flat_r):
     n_exp, dim, ff = up.shape
     tok = x_hbm.shape[0]
     chips = side * side
@@ -49,7 +58,7 @@
 
     x_loads = [pltpu.make_async_copy(x_hbm.at[:, pl.ds(k * kw, kw)], gath.at[k, core, 0], in_sem.at[0]) for k in range(KC)]
     loads = [pltpu.make_async_copy(ids_hbm, ids_v, in_sem.at[1]), pltpu.make_async_copy(gates_hbm, gates_v, in_sem.at[2])]
-    for c in loads + x_loads:
+    for c in x_loads + loads:
         c.start()
     barrier = pltpu.get_barrier_semaphore()
     for dy, dx in offs:
@@ -64,7 +73,11 @@
     pltpu.make_async_copy(gath.at[:, core, 0], gath.at[:, core, 0], in_sem.at[0]).wait()
 
     def up_copy(k):
-        return pltpu.make_async_copy(up_hbm.at[:, pl.ds(k * kw, kw), :], up.at[:, pl.ds(k * kw, kw), :], up_sem.at[k])
+        s = pl.ds(k * kw, kw)
+        return pltpu.make_async_copy(up_hbm.at[:, s], up.at[:, s], up_sem.at[k])
+
+    def up_wait(k):
+        up_copy(k).wait()
 
     def down_copy(q):
         return pltpu.make_async_copy(down_hbm.at[:, :, pl.ds(q * qw, qw)], down.at[:, :, pl.ds(q * qw, qw)], down_sem.at[q])
@@ -75,26 +88,24 @@
         down_copy(q).start()
     pl.semaphore_wait(barrier, len(offs) + 1)
 
-    def block(k):
-        return meta if k == KC else gath.at[k]
+    block = [meta] + [gath.at[k] for k in range(KC)]
+    streams = range(KC + 1)
 
     def send(k, o):
-        b = block(k)
+        b = block[k]
         return rcopy(b.at[core, 0], b.at[core, neg(o[0]) * side + neg(o[1])], ag_s.at[k], ag_r.at[k], at(*o))
 
     def gathered(k):
-        b = block(k).at[core, pl.ds(1, chips - 1)]
+        b = block[k].at[core, pl.ds(1, chips - 1)]
         return rcopy(b, b, ag_s.at[k], ag_r.at[k], partner)
 
     def forward(k):
-        b = block(k).at[core]
+        b = block[k].at[core]
         return rcopy(b, b, fw_s.at[k], fw_r.at[k], partner)
 
     def forwarded(k):
-        b = block(k).at[1 - core]
+        b = block[k].at[1 - core]
         return rcopy(b, b, fw_s.at[k], fw_r.at[k], partner)
-
-    streams = [KC] + list(range(KC))
 
     @pl.when(core == 1)
     def _():
@@ -106,10 +117,9 @@
 
     @pl.when(core == 0)
     def _():
-        for k in streams[:-1]:
+        for k in range(GO):
             gathered(k).wait_send()
         pl.semaphore_signal(go, inc=1, device_id=partner, device_id_type=MESH)
-        gathered(streams[-1]).wait_send()
 
     def pass_on(k):
         gathered(k).wait_recv()
@@ -135,6 +145,8 @@
             gate[c, e] = jnp.broadcast_to(g, (half, LANES))
 
     def up_chunk(c, k):
+        if k == 0:
+            find_gates(c)
         rows[k] = gath[k, c].astype(jnp.float32).reshape(half, kw).astype(jnp.bfloat16)
         for e in range(n_exp):
             acc = jnp.dot(rows[k], up[e, pl.ds(k * kw, kw), :], preferred_element_type=jnp.float32)
@@ -143,7 +155,7 @@
             if k < KC - 1:
                 z[e] = acc
             else:
-                act = jax.nn.gelu(acc, approximate=True)
+                act = gelu(acc)
                 h[e] = jnp.where(wide(gate[c, e], ff) > 0.0, act, 0.0).astype(jnp.bfloat16)
 
     def down_chunk(c, q):
@@ -153,8 +165,9 @@
             o = o.reshape(side, side, tok, qw)
             part[c, q] = o if e == 0 else part[c, q] + o
 
-    def pair_out(c, q):
-        return rcopy(part.at[c, q], pair.at[q], pair_s, pair_r.at[q], partner)
+    def pair_out(c, qs):
+        r = pl.ds(qs[0], len(qs))
+        return rcopy(part.at[c, r], pair.at[r], pair_s, pair_r.at[qs[0]], partner)
 
     def ring_out(c, q, d):
         lane = q % 2 == 0
@@ -168,11 +181,18 @@
     def came(ref, ss, rs):
         return rcopy(ref, ref, ss, rs, partner)
 
-    def stage1(c, q):
-        came(pair.at[q], pair_s, pair_r.at[q]).wait_recv()
-        part[c, q] = part[c, q] + pair[q]
-        for d in line_offs:
-            ring_out(c, q, d).start()
+    def stage1(c, qs):
+        came(pair.at[pl.ds(qs[0], len(qs))], pair_s, pair_r.at[qs[0]]).wait_recv()
+        for q in qs:
+            part[c, q] = part[c, q] + pair[q]
+        for q in qs:
+            if c == 1 and q in direct:
+                for o in offs:
+                    i, j = neg(o[0]), neg(o[1])
+                    rcopy(part.at[c, q, o[0], o[1]], flat.at[i * side + j], flat_s, flat_r, at(*o)).start()
+            else:
+                for d in line_offs:
+                    ring_out(c, q, d).start()
 
     def stage2(c, q):
         came(ring.at[q, pl.ds(1, side - 1)], ring_s, ring_r.at[q]).wait_recv()
@@ -185,81 +205,97 @@
 
     def stage3(q):
         came(cross.at[q, pl.ds(1, side - 1)], cross_s, cross_r.at[q]).wait_recv()
-        s = line[q, 0]
+        t = line[q, 0]
         for d in range(1, side):
-            s = s + cross[q, d]
-        y_ref[:, q * qw:(q + 1) * qw] = s.astype(y_ref.dtype)
-
-    arrive(0, KC)
-    find_gates(0)
+            t = t + cross[q, d]
+        y_ref[:, q * qw:(q + 1) * qw] = t.astype(y_ref.dtype)
+
+    def stage_flat(q):
+        came(flat.at[pl.ds(1, chips - 1)], flat_s, flat_r).wait_recv()
+        t = part[1, q, 0, 0]
+        for j in range(1, chips):
+            t = t + flat[j]
+        y_ref[:, q * qw:(q + 1) * qw] = t.astype(y_ref.dtype)
+
+    direct = (QC - 1,) if FLAT else ()
+    rest = [q for q in range(QC) if q not in direct]
+
+    arrive(0, 0)
     for k in range(KC):
-        arrive(0, k)
-        up_copy(k).wait()
+        arrive(0, k + 1)
+        up_wait(k)
         up_chunk(0, k)
-    pending = list(streams)
-
-    def next_pass(n):
-        ks, pending[:] = pending[:n], pending[n:]
-        for k in ks:
-            pass_on(k)
-
-    @pl.when(core == 1)
-    def _():
-        next_pass(2)
-    for q in range(QC):
-        down_copy(q).wait()
-        down_chunk(0, q)
-
+    for i, qs in enumerate(BLOCKS[0]):
         @pl.when(core == 1)
         def _():
-            pair_out(0, q).start()
-            next_pass(1 if q < QC - 1 else len(pending))
-
-    arrive(1, KC)
-    find_gates(1)
+            for k in PASS[i]:
+                pass_on(k)
+        for q in qs:
+            down_copy(q).wait()
+        for q in qs:
+            down_chunk(0, q)
+
+        @pl.when(core == 1)
+        def _():
+            pair_out(0, qs).start()
+
+    arrive(1, 0)
     for k in range(KC):
-        arrive(1, k)
+        arrive(1, k + 1)
         up_chunk(1, k)
-        if k < QC:
+        if True:
             @pl.when(core == 0)
             def _():
-                stage1(0, k)
-    for q in range(QC):
-        down_chunk(1, q)
+                stage1(0, BLOCKS[0][k])
+    for i, qs in enumerate(BLOCKS[1]):
+        for q in qs:
+            down_chunk(1, q)
 
         @pl.when(core == 0)
         def _():
-            pair_out(1, q).start()
-            if q >= 1:
-                stage2(0, q - 1)
+            pair_out(1, qs).start()
 
         @pl.when(core == 1)
         def _():
-            if q >= LAG:
-                stage1(1, q - LAG)
+            stage1(1, qs)
 
     @pl.when(core == 0)
     def _():
-        stage2(0, QC - 1)
+        for q in range(QC):
+            stage2(0, q)
+        for q in range(QC):
+            stage3(q)
 
     @pl.when(core == 1)
     def _():
-        for q in range(QC - LAG, QC):
-            stage1(1, q)
-        for q in range(QC):
+        for q in rest:
             stage2(1, q)
-    for q in range(QC):
-        stage3(q)
-
-    @pl.when(core == 1)
-    def _():
-        for k in streams:
+        for q in direct:
+            stage_flat(q)
+        for q in rest:
+            stage3(q)
+        for k in range(GO):
             gathered(k).wait_send()
+
+    for k in range(GO, KC + 1):
+        gathered(k).wait_send()
     for k in streams:
         forward(k).wait_send()
-    came(pair, pair_s, pair_r.at[0]).wait_send()
-    came(ring.at[:, pl.ds(1, side - 1)], ring_s, ring_r.at[0]).wait_send()
-    came(cross.at[:, pl.ds(1, side - 1)], cross_s, cross_r.at[0]).wait_send()
+
+    @pl.when(core == 0)
+    def _():
+        came(pair, pair_s, pair_r.at[0]).wait_send()
+        came(ring.at[:, pl.ds(1, side - 1)], ring_s, ring_r.at[0]).wait_send()
+        came(cross.at[:, pl.ds(1, side - 1)], cross_s, cross_r.at[0]).wait_send()
+
+    @pl.when(core == 1)
+    def _():
+        n = len(rest)
+        came(pair, pair_s, pair_r.at[0]).wait_send()
+        came(ring.at[pl.ds(0, n), pl.ds(1, side - 1)], ring_s, ring_r.at[0]).wait_send()
+        came(cross.at[pl.ds(0, n), pl.ds(1, side - 1)], cross_s, cross_r.at[0]).wait_send()
+        if direct:
+            came(flat.at[pl.ds(1, chips - 1)], flat_s, flat_r).wait_send()
 
 
 def solution(mesh):
@@ -272,17 +308,17 @@
         tok, dim = x_loc.shape
         n_exp, _, ff = w_up.shape
         half = tok * group // 2
-        kw, qw = dim // KC, dim // QC
+        qw = dim // QC
         f32, bf16 = jnp.float32, jnp.bfloat16
         dma = pltpu.SemaphoreType.DMA
         scratch = [
             pltpu.VMEM(w_up.shape, bf16),
             pltpu.VMEM(w_down.shape, bf16),
-            pltpu.VMEM((KC, 2, side * side, tok, kw), bf16),
+            pltpu.VMEM((KC, 2, side * side, tok, dim // KC), bf16),
             pltpu.VMEM((2, side * side, tok, LANES), f32),
             pltpu.VMEM(ids_loc.shape, jnp.int32),
             pltpu.VMEM(gates_loc.shape, f32),
-            pltpu.VMEM((KC, half, kw), bf16),
+            pltpu.VMEM((KC, half, dim // KC), bf16),
             pltpu.VMEM((n_exp, half, ff), f32),
             pltpu.VMEM((n_exp, half, ff), bf16),
             pltpu.VMEM((2, n_exp, half, LANES), f32),
@@ -291,13 +327,14 @@
             pltpu.VMEM((QC, side, side, tok, qw), f32),
             pltpu.VMEM((QC, side, tok, qw), f32),
             pltpu.VMEM((QC, side, tok, qw), f32),
+            pltpu.VMEM((side * side, tok, qw), f32),
             dma((3,)), dma((KC,)), dma((QC,)), pltpu.SemaphoreType.REGULAR,
             dma((KC + 1,)), dma((KC + 1,)), dma((KC + 1,)), dma((KC + 1,)),
-            dma, dma((QC,)), dma, dma((QC,)), dma, dma((QC,)),
+            dma, dma((QC,)), dma, dma((QC,)), dma, dma((QC,)), dma, dma,
         ]
         return pl.pallas_call(
             functools.partial(moe_kernel, side),
-            out_shape=jax.ShapeDtypeStruct((tok, dim), bf16),
+            out_shape=pltpu.VMEM((tok, dim), bf16),
             in_specs=[pl.BlockSpec(memory_space=pl.ANY)] * 5,
             out_specs=pl.BlockSpec(memory_space=pltpu.VMEM),
             scratch_shapes=scratch,

time: 37.8 us -> 34.8 us (0.921)
  Pallas kernels: 36.2 us -> 34 us
  local copies, waits for them, and re-layouts: 1.38 us -> 0.62 us
    pallas_call x1, Pallas kernels: 36.2 us -> 34 us  [local_layer(): pl.pallas_call(functools.partial(moe_kernel, side), out_shape=pltpu.VMEM(...]
    unnamed x1, local copies, waits for them, and re-layouts: 1.38 us -> 0.62 us
where the time goes in v3:
time: 34.8 us; the launch traced here: 34.7 us
  Pallas kernels  34 us (98%)
  local copies, waits for them, and re-layouts  0.62 us (2%)
    pallas_call x1, Pallas kernels, local_layer(): pl.pallas_call(functools.partial(moe_kernel, side), out_shape=pltpu.VMEM(...  34 us

profile of v3, /device:TPU:97, one launch (start us, length us, event | category | flops | bytes accessed | tf_op | source)
XLA Modules:
  0.0 34.7 jit_solution(9705342135775419998)
XLA Ops:
  0.0 34.0 %shard_map.55 = bf16[8,2048]{1,0:T(8,128)(2,1)S(1)} custom-call(bf16[8,2048]{1,0:T(8,128)(2,1)} %x_hbm.1, s32[8,8]{1,0:T(8,128)} %ids_hbm.1, f32[8,8]{1,0:T(8,128)} %gates_hbm.1, bf16[8,2048,512]{2,1,0:T(8,128)(2,1)} %up_hbm.1, bf16[8,512,2048]{2,1,0:T(8,128)(2,1)} %down_hbm.1), custom_call_target="tpu_custom_call" | custom-call | tf_op jit(solution)/shard_map/pallas_call | solution.py:335
  34.0 0.6 %copy.7 = bf16[8,2048]{1,0:T(8,128)(2,1)} copy(bf16[8,2048]{1,0:T(8,128)(2,1)S(1)} %shard_map.55) | data formatting | bytes 65536

commit v4 on v3

--- a/solution.py
+++ b/solution.py
@@ -74,10 +74,11 @@
 
     def up_copy(k):
         s = pl.ds(k * kw, kw)
-        return pltpu.make_async_copy(up_hbm.at[:, s], up.at[:, s], up_sem.at[k])
+        return pltpu.make_async_copy(up_hbm.at[:, s], up.at[:, s], up_sem)
 
     def up_wait(k):
-        up_copy(k).wait()
+        if k == 0:
+            pltpu.make_async_copy(up_hbm, up, up_sem).wait()
 
     def down_copy(q):
         return pltpu.make_async_copy(down_hbm.at[:, :, pl.ds(q * qw, qw)], down.at[:, :, pl.ds(q * qw, qw)], down_sem.at[q])
@@ -101,11 +102,11 @@
 
     def forward(k):
         b = block[k].at[core]
-        return rcopy(b, b, fw_s.at[k], fw_r.at[k], partner)
+        return rcopy(b, b, fw_s.at[min(k, 1)], fw_r.at[k], partner)
 
     def forwarded(k):
         b = block[k].at[1 - core]
-        return rcopy(b, b, fw_s.at[k], fw_r.at[k], partner)
+        return rcopy(b, b, fw_s.at[min(k, 1)], fw_r.at[k], partner)
 
     @pl.when(core == 1)
     def _():
@@ -254,6 +255,8 @@
         @pl.when(core == 0)
         def _():
             pair_out(1, qs).start()
+            if i >= 2:
+                stage2(0, i - 2)
 
         @pl.when(core == 1)
         def _():
@@ -261,7 +264,7 @@
 
     @pl.when(core == 0)
     def _():
-        for q in range(QC):
+        for q in range(2, QC):
             stage2(0, q)
         for q in range(QC):
             stage3(q)
@@ -280,7 +283,10 @@
     for k in range(GO, KC + 1):
         gathered(k).wait_send()
     for k in streams:
-        forward(k).wait_send()
+        if k == 0:
+            forward(k).wait_send()
+    x_all = gath.at[:, core]
+    rcopy(x_all, x_all, fw_s.at[1], fw_r.at[1], partner).wait_send()
 
     @pl.when(core == 0)
     def _():
@@ -328,8 +334,8 @@
             pltpu.VMEM((QC, side, tok, qw), f32),
             pltpu.VMEM((QC, side, tok, qw), f32),
             pltpu.VMEM((side * side, tok, qw), f32),
-            dma((3,)), dma((KC,)), dma((QC,)), pltpu.SemaphoreType.REGULAR,
-            dma((KC + 1,)), dma((KC + 1,)), dma((KC + 1,)), dma((KC + 1,)),
+            dma((3,)), dma, dma((QC,)), pltpu.SemaphoreType.REGULAR,
+            dma((KC + 1,)), dma((KC + 1,)), dma((2,)), dma((KC + 1,)),
             dma, dma((QC,)), dma, dma((QC,)), dma, dma((QC,)), dma, dma,
         ]
         return pl.pallas_call(

time: 34.8 us -> 36.5 us (1.049)
  Pallas kernels: 34 us -> 35.8 us
    pallas_call x1, Pallas kernels: 34 us -> 35.8 us  [local_layer(): pl.pallas_call(functools.partial(moe_kernel, side), out_shape=pltpu.VMEM(...]
where the time goes in v4:
time: 36.5 us; the launch traced here: 36.4 us
  Pallas kernels  35.8 us (98%)
  local copies, waits for them, and re-layouts  0.62 us (2%)
    pallas_call x1, Pallas kernels, local_layer(): pl.pallas_call(functools.partial(moe_kernel, side), out_shape=pltpu.VMEM(...  35.8 us

profile of v4, /device:TPU:97, one launch (start us, length us, event | category | flops | bytes accessed | tf_op | source)
XLA Modules:
  0.0 36.4 jit_solution(14989047095738068977)
XLA Ops:
  0.0 35.8 %shard_map.55 = bf16[8,2048]{1,0:T(8,128)(2,1)S(1)} custom-call(bf16[8,2048]{1,0:T(8,128)(2,1)} %x_hbm.1, s32[8,8]{1,0:T(8,128)} %ids_hbm.1, f32[8,8]{1,0:T(8,128)} %gates_hbm.1, bf16[8,2048,512]{2,1,0:T(8,128)(2,1)} %up_hbm.1, bf16[8,512,2048]{2,1,0:T(8,128)(2,1)} %down_hbm.1), custom_call_target="tpu_custom_call" | custom-call | tf_op jit(solution)/shard_map/pallas_call | solution.py:341
  35.8 0.6 %copy.7 = bf16[8,2048]{1,0:T(8,128)(2,1)} copy(bf16[8,2048]{1,0:T(8,128)(2,1)S(1)} %shard_map.55) | data formatting | bytes 65536
